TPU v7x, 32 devices: a whole 2x2x4 slice. The times are simulated.
32 devices in a mesh: section: 4 (over x, core), ep: 8 (over z, y).
Axes of the slice: x: 2, y: 2, z: 4, core: 2. Of those that a mesh axis runs over, the one named last changes fastest.
Arguments:
- hidden_states: bfloat16 [384, 6144], P('ep'), may hold values from -6 to 6
- route_experts: int32 [384, 2], P('ep'), may hold values from 0 to 7, all different within a row; in each aligned block of 48 rows (0 to 47, 48 to 95, ...) at most 24 rows name the same one
- route_weights: float32 [384, 2], P('ep'), may hold values from 0.05 to 1
- gate_weight: bfloat16 [8, 6144, 8192], P('ep', None, 'section'), may hold values from -0.078125 to 0.078125
- up_weight: bfloat16 [8, 6144, 8192], P('ep', None, 'section'), may hold values from -0.078125 to 0.078125
- down_weight: bfloat16 [8, 8192, 6144], P('ep', 'section'), may hold values from -0.0625 to 0.0625
Outputs:
- layer_out: bfloat16 [384, 6144], P('ep', 'section')
Inputs may be any that keep to these rules, and one draw needn't show every extreme that they name: `route_experts`: each row names two different experts. Among the 48 rows of one ep index no expert is named by more than 24 rows, and in every draw some expert is named by exactly 24 rows of some ep index.
All inputs are finite; a program needn't handle non-finite values.
Results may differ from a plain program's by a relative error of at most 0.015.
Values may be sent and summed in bfloat16 or wider, within the bound.
A program may use at most 128 MiB of HBM per device.

v0:
```python
import jax
import jax.numpy as jnp
from jax import lax
from jax.sharding import PartitionSpec as P

EXPERTS = 8


def expert_rows(incoming, gate_weight, up_weight, down_weight):
    sources, slot_count, features = incoming.shape
    stacked = incoming.reshape(sources * slot_count, features)
    gate_value = jnp.dot(stacked, gate_weight[0], preferred_element_type=jnp.float32)
    up_value = jnp.dot(stacked, up_weight[0], preferred_element_type=jnp.float32)
    hidden = (jax.nn.silu(gate_value) * up_value).astype(jnp.bfloat16)
    result = jnp.dot(hidden, down_weight[0], preferred_element_type=jnp.float32).astype(
        jnp.bfloat16
    )
    return result.reshape(sources, slot_count, features)


def on_device(hidden_states, route_experts, route_weights, gate_weight, up_weight, down_weight):
    ep_count = lax.axis_size("ep")
    section_count = lax.axis_size("section")
    tok_rows, features = hidden_states.shape
    members = ep_count // EXPERTS
    capacity = tok_rows // 2
    chosen = route_experts.reshape(-1)
    one_hot = (chosen[:, None] == jnp.arange(EXPERTS, dtype=jnp.int32)[None, :]).astype(jnp.int32)
    earlier = jnp.cumsum(one_hot, axis=0) - one_hot
    slot_index = jnp.sum(earlier * one_hot, axis=1)
    position = (chosen * capacity + slot_index).reshape(tok_rows, 2)
    columns = jnp.arange(EXPERTS * capacity, dtype=jnp.int32)
    matches = position[:, :, None] == columns[None, None, :]
    select = jnp.sum(matches.astype(jnp.int32), axis=1).astype(jnp.bfloat16)
    weighing = jnp.sum(matches.astype(jnp.float32) * route_weights[:, :, None], axis=1)
    packed = jnp.einsum(
        "tj,td->jd", select, hidden_states, preferred_element_type=jnp.float32
    ).astype(jnp.bfloat16)
    outgoing = jnp.repeat(packed.reshape(EXPERTS, capacity, features), members, axis=0)
    slot_share = capacity // section_count
    first_slot = lax.axis_index("section") * slot_share
    own_slots = lax.dynamic_slice_in_dim(outgoing, first_slot, slot_share, 1)
    arrived = lax.all_to_all(own_slots, "ep", split_axis=0, concat_axis=0, tiled=True)
    partials = expert_rows(
        lax.all_gather(arrived, "section", axis=1, tiled=True), gate_weight, up_weight, down_weight
    )
    summed = lax.psum_scatter(
        partials.astype(jnp.float32).astype(jnp.bfloat16),
        "section",
        scatter_dimension=1,
        tiled=True,
    ).astype(jnp.float32)
    returned = lax.all_to_all(
        summed.astype(jnp.bfloat16), "ep", split_axis=0, concat_axis=0, tiled=True
    ).astype(summed.dtype)
    merged = jnp.sum(returned.reshape(EXPERTS, members, slot_share, features), axis=1)
    weigh_part = lax.dynamic_slice_in_dim(
        weighing.reshape(tok_rows, EXPERTS, capacity), first_slot, slot_share, 2
    )
    contribution = jnp.dot(
        weigh_part.reshape(tok_rows, EXPERTS * slot_share),
        merged.reshape(EXPERTS * slot_share, features),
        precision=lax.Precision.HIGHEST,
        preferred_element_type=jnp.float32,
    )
    layer_out = lax.psum_scatter(
        contribution.astype(jnp.bfloat16), "section", scatter_dimension=1, tiled=True
    )
    return layer_out


def solution(mesh):
    return jax.shard_map(
        on_device,
        mesh=mesh,
        in_specs=(
            P("ep", None),
            P("ep", None),
            P("ep", None),
            P("ep", None, "section"),
            P("ep", None, "section"),
            P("ep", "section", None),
        ),
        out_specs=P("ep", "section"),
        check_vma=False,
    )
```

profile of v0, /device:TPU:0, one launch (start us, length us, event | category | flops | bytes accessed | tf_op | source)
XLA Modules:
  0.0 190.9 jit_solution(7854758130795143767)
XLA Ops:
  6.5 0.8 copy.54
  7.4 0.1 eq.28
  7.5 0.1 fusion.25
  7.6 0.1 reduce_window_sum.11
  7.7 0.2 select_reduce_fusion.1
  7.9 0.1 reduce_sum.34
  8.1 0.7 multiply_add_fusion
  8.9 0.8 convolution_convert_fusion
  9.7 0.2 constant_dynamic-slice_fusion.1
  9.9 27.3 %all_to_all.10 = bf16[8,6,6144]{2,1,0:T(8,128)(2,1)S(1)} all-to-all(bf16[8,6,6144]{2,1,0:T(8,128)(2,1)S(1)} %constant_dynamic-slice_fusion.1), channel_id=1, replica_groups=mesh['section'=4,'ep'=8] {'ep'}, dimensions={0} | all-to-all | bytes 1179648 | tf_op jit(solution)/shard_map/all_to_all | solution.py:43
  37.2 1.2 copy.58
  38.4 23.2 %all-gather.2.cloned.1.call-done = bf16[8,24,6144]{2,0,1:T(8,128)(2,1)} async-done(((bf16[8,6,6144]{2,0,1:T(8,128)(2,1)}), bf16[8,24,6144]{2,0,1:T(8,128)(2,1)}) %all-gather.2.cloned.1.call-update) | async-done | bytes 2359312 | tf_op jit(solution)/shard_map/all_gather | solution.py:45
  61.6 3.0 %copy.59 = bf16[8,24,6144]{2,1,0:T(8,128)(2,1)S(1)} copy(bf16[8,24,6144]{2,0,1:T(8,128)(2,1)} %all-gather.2.cloned.1.call-done) | data formatting | bytes 4718592 | tf_op jit(solution)/shard_map/all_gather | solution.py:45
  64.6 12.0 %fusion.4 = f32[192,2048]{1,0:T(8,128)} fusion(bf16[192,6144]{1,0:T(8,128)(2,1)S(1)} %bitcast.29, bf16[1,6144,2048]{2,1,0:T(8,128)(2,1)} %param.9), kind=kOutput, calls=%fused_computation.4 | convolution fusion | flops 4831838208 | bytes 29097984 | tf_op jit(solution)/shard_map/dot_general | solution.py:12
  76.5 20.7 %fusion.6 = bf16[192,6144]{1,0:T(8,128)(2,1)} fusion(bf16[1,2048,6144]{2,1,0:T(8,128)(2,1)} %param.11, bf16[192,6144]{1,0:T(8,128)(2,1)S(1)} %bitcast.30, bf16[1,6144,2048]{2,1,0:T(8,128)(2,1)} %param.10, f32[192,2048]{1,0:T(8,128)} %fusion.4), kind=kOutput, calls=%fused_computation.6 | convolution fusion | flops 9667215360 | bytes 56623104 | tf_op jit(solution)/shard_map/dot_general | solution.py:15
  97.3 4.4 %copy.60 = bf16[8,24,6144]{2,0,1:T(8,128)(2,1)} copy(bf16[8,24,6144]{2,1,0:T(8,128)(2,1)} %bitcast.31) | data formatting | bytes 4718592 | tf_op jit(solution)/shard_map/reshape | solution.py:18
  101.7 33.0 %reduce-scatter.3.cloned.1.call-done = bf16[8,6,6144]{2,0,1:T(8,128)(2,1)} async-done(((bf16[8,24,6144]{2,0,1:T(8,128)(2,1)}), bf16[8,6,6144]{2,0,1:T(8,128)(2,1)}) %reduce-scatter.3.cloned.1.call-update) | async-done | bytes 589840 | tf_op jit(solution)/shard_map/reduce_scatter | solution.py:47
  134.6 2.3 %copy.61 = bf16[8,6,6144]{2,1,0:T(8,128)(2,1)} copy(bf16[8,6,6144]{2,0,1:T(8,128)(2,1)} %reduce-scatter.3.cloned.1.call-done) | data formatting | bytes 1179648 | tf_op jit(solution)/shard_map/reduce_scatter | solution.py:47
  136.9 5.5 %all-to-all-start.1 = ((bf16[8,6,6144]{2,1,0:T(8,128)(2,1)}), bf16[8,6,6144]{2,1,0:T(8,128)(2,1)S(1)}, u32[]{:S(2)}, u32[]{:S(2)}) async-start(bf16[8,6,6144]{2,1,0:T(8,128)(2,1)} %copy.61), calls=%async_computation.2 | async-start | bytes 1572864 | tf_op jit(solution)/shard_map/all_to_all | solution.py:53
  142.5 0.1 select_reduce_fusion
  142.6 0.1 copy.56
  142.7 19.8 %all-to-all-done.1 = bf16[8,6,6144]{2,1,0:T(8,128)(2,1)S(1)} async-done(((bf16[8,6,6144]{2,1,0:T(8,128)(2,1)}), bf16[8,6,6144]{2,1,0:T(8,128)(2,1)S(1)}, u32[]{:S(2)}, u32[]{:S(2)}) %all-to-all-start.1) | async-done | bytes 589856 | tf_op jit(solution)/shard_map/all_to_all | solution.py:53
  162.5 1.7 fusion.9
  164.2 20.2 %reduce-scatter.5.cloned.1.call-done = bf16[48,1536]{1,0:T(8,128)(2,1)} async-done(((bf16[48,6144]{1,0:T(8,128)(2,1)}), bf16[48,1536]{1,0:T(8,128)(2,1)}) %reduce-scatter.5.cloned.1.call-update) | async-done | bytes 147472 | tf_op jit(solution)/shard_map/reduce_scatter | solution.py:66
  (15 shorter events, 0.3 us)
Async XLA Ops:
  6.5 2.4 %copy-start = (bf16[48,6144]{1,0:T(8,128)(2,1)S(1)}, bf16[48,6144]{1,0:T(8,128)(2,1)}, u32[]{:S(2)}) copy-start(bf16[48,6144]{1,0:T(8,128)(2,1)} %param.6) | copy-start | bytes 1769476
  6.5 55.1 %all-gather.2.cloned.1.call-start = ((), (), s32[]{:S(2)}) async-start(), calls=%async_computation.4 | async-start | bytes 2949120 | tf_op jit(solution)/shard_map/all_gather | solution.py:45
  38.4 96.3 %reduce-scatter.3.cloned.1.call-start = ((), (), s32[]{:S(2)}) async-start(), calls=%async_computation.5 | async-start | bytes 2949120 | tf_op jit(solution)/shard_map/reduce_scatter | solution.py:47
  101.6 40.8 %copy-start.2 = (f32[48,2]{0,1:T(2,128)S(1)}, f32[48,2]{0,1:T(2,128)}, u32[]{:S(2)}) copy-start(f32[48,2]{0,1:T(2,128)} %param.8) | copy-start | bytes 1156
  101.7 82.7 %copy-start.1 = (bf16[48,6144]{1,0:T(8,128)(2,1)S(1)}, bf16[48,6144]{1,0:T(8,128)(2,1)}, u32[]{:S(2)}) copy-start(bf16[48,6144]{1,0:T(8,128)(2,1)} %param.6) | copy-start | bytes 1769476
  136.9 25.6 %all-to-all-start.1 = ((bf16[8,6,6144]{2,1,0:T(8,128)(2,1)}), bf16[8,6,6144]{2,1,0:T(8,128)(2,1)S(1)}, u32[]{:S(2)}, u32[]{:S(2)}) async-start(bf16[8,6,6144]{2,1,0:T(8,128)(2,1)} %copy.61), calls=%async_computation.2 | async-start | bytes 1572864 | tf_op jit(solution)/shard_map/all_to_all | solution.py:53
  142.4 42.0 %reduce-scatter.5.cloned.1.call-start = ((), (), s32[]{:S(2)}) async-start(), calls=%async_computation.6 | async-start | bytes 737280 | tf_op jit(solution)/shard_map/reduce_scatter | solution.py:66
Sparse Core Ops, SparseCore 0:
  38.5 23.0 all-gather.1
  101.8 32.8 reduce-scatter.2
  164.4 20.0 reduce-scatter.4
where the time goes:
time: 191 us
  waiting for transfers between devices  96.1 us (50%)
  matrix products  35.2 us (18%)
  blocking collectives  27.3 us (14%)
  between operations  13.2 us (7%)
  local copies, waits for them, and re-layouts  12.3 us (6%)
  starting transfers between devices  5.6 us (3%)
    reduce_scatter x1, waiting for transfers between devices, on_device(): lax.psum_scatter(partials.astype(jnp.float32).astype(jnp.bfloat16), 'sect...  33 us
    all_to_all x1, blocking collectives, on_device(): lax.all_to_all(own_slots, 'ep', split_axis=0, concat_axis=0, tiled=True)  27.3 us
    all_gather x1, waiting for transfers between devices, on_device(): lax.all_gather(arrived, 'section', axis=1, tiled=True)  23.2 us
    dot_general x1, matrix products, expert_rows(): jnp.dot(hidden, down_weight[0], preferred_element_type=jnp.float32)  20.7 us
    reduce_scatter x1, waiting for transfers between devices, on_device(): lax.psum_scatter(contribution.astype(jnp.bfloat16), 'section', scatter_di...  20.2 us
    all_to_all x1, waiting for transfers between devices, on_device(): lax.all_to_all(summed.astype(jnp.bfloat16), 'ep', split_axis=0, concat_ax...  19.8 us
    dot_general x1, matrix products, expert_rows(): jnp.dot(stacked, gate_weight[0], preferred_element_type=jnp.float32)  12 us
    all_to_all x1, starting transfers between devices, on_device(): lax.all_to_all(summed.astype(jnp.bfloat16), 'ep', split_axis=0, concat_ax...  5.52 us
  transfers between devices with their start and end apart: 4, of which 4 were waited for; matrix products, arithmetic and copies ran while one was open for 0% of the time, Pallas kernels for 0%

commit v1 on v0

v1 whole, which is shorter than its diff:
```python
import functools

import jax
import jax.numpy as jnp
from jax import lax
from jax.experimental import pallas as pl
from jax.experimental.pallas import tpu as pltpu
from jax.sharding import PartitionSpec as P

EXPERTS = 8
CORES = 2
MESH = pl.DeviceIdType.MESH


def fit(size, options):
    return next(o for o in options if size % o == 0)


def kernel(
    E, S, C, D, FFS, tf, ft, NG, ND,
    packed, weigh, gate, up, down, out,
    x_all, gbuf, ubuf, dbuf, hid, psend, prec, pmine, xsend, xrec, own, sumb, ret,
    s1, r1, s2, r2, s3, r3, s4, r4, s5, r5, s6, r6, gs, us, ds, lsem,
):
    nx = S // CORES
    M = E // EXPERTS
    DS = D // S
    NT = DS // ft
    NTF = FFS // tf
    R = E * C
    sec = lax.axis_index("section")
    me = lax.axis_index("ep")
    x, c = sec // CORES, lax.rem(sec, CORES)
    mate = x * CORES + 1 - c
    f32 = jnp.float32

    def gcopy(t):
        slot = lax.rem(t, NG)
        cols = pl.ds(pl.multiple_of(t * tf, tf), tf)
        return (
            pltpu.make_async_copy(gate.at[0, :, cols], gbuf.at[slot], gs.at[slot]),
            pltpu.make_async_copy(up.at[0, :, cols], ubuf.at[slot], us.at[slot]),
        )

    def dcopy(q):
        slot = lax.rem(q, ND)
        xi, f, ci = q // (NT * CORES), lax.rem(q // CORES, NT), lax.rem(q, CORES)
        xd = lax.rem(x + 1 + xi, nx)
        cd = (1 - c) * (1 - ci) + c * ci
        start = (xd * CORES + cd) * DS + f * ft
        cols = pl.ds(pl.multiple_of(start, 128), ft)
        return pltpu.make_async_copy(down.at[0, :, cols], dbuf.at[slot], ds.at[slot])

    for t in range(min(NG, NTF)):
        for cp in gcopy(t):
            cp.start()
    local = pltpu.make_async_copy(packed.at[me // M], x_all.at[sec, me], lsem)
    local.start()

    barrier = pltpu.get_barrier_semaphore()

    def greet(k, _):
        pl.semaphore_signal(barrier, inc=1, device_id=(sec, lax.rem(me + k, E)), device_id_type=MESH)
        return 0

    lax.fori_loop(1, E, greet, 0)
    for j in range(1, nx):
        pl.semaphore_signal(
            barrier, inc=1, device_id=(lax.rem(x + j, nx) * CORES + c, me), device_id_type=MESH
        )
    pl.semaphore_signal(barrier, inc=1, device_id=(mate, me), device_id_type=MESH)
    pl.semaphore_wait(barrier, E - 1 + nx)

    def rcopy(src, dst, ss, rs, dev):
        return pltpu.make_async_remote_copy(
            src_ref=src, dst_ref=dst, send_sem=ss, recv_sem=rs, device_id=dev, device_id_type=MESH
        )

    def c1(k):
        dst = lax.rem(me + k, E)
        return rcopy(packed.at[dst // M], x_all.at[sec, me], s1.at[k], r1.at[k], (sec, dst))

    def c2(j, k):
        src = lax.rem(me - k + E, E)
        piece = x_all.at[sec, src]
        return rcopy(
            piece, piece, s2.at[j, k], r2.at[j, k], (lax.rem(x + j, nx) * CORES + c, me)
        )

    def c3(j, k):
        src = lax.rem(me - k + E, E)
        piece = x_all.at[lax.rem(x - j + nx, nx) * CORES + c, src]
        return rcopy(piece, piece, s3.at[j, k], r3.at[j, k], (mate, me))

    def loop(lo, hi, body):
        def step(i, carry):
            body(i)
            return carry

        lax.fori_loop(lo, hi, step, 0)

    loop(1, E, lambda k: c1(k).start())
    for q in range(min(ND, nx * NT * CORES)):
        dcopy(q).start()

    def spread(k):
        for j in range(1, nx):
            c2(j, k).start()
        c3(0, k).start()

    def relay(k):
        for j in range(1, nx):
            c2(j, k).wait_recv()
            c3(j, k).start()

    local.wait()
    spread(0)

    def forward(k):
        c1(k).wait_recv()
        spread(k)
        relay(k - 1)

    loop(1, E, forward)
    relay(E - 1)

    def settle(k):
        for j in range(nx):
            c3(j, k).wait()
        for j in range(1, nx):
            c2(j, k).wait_send()

    loop(0, E, settle)
    loop(1, E, lambda k: c1(k).wait_send())

    def hidden_tile(t):
        slot = lax.rem(t, NG)
        for cp in gcopy(t):
            cp.wait()
        g = jnp.zeros((R, tf), f32)
        u = jnp.zeros((R, tf), f32)
        for s in range(S):
            rows = x_all[s].reshape(R, DS)
            g += jnp.dot(rows, gbuf[slot, s * DS:(s + 1) * DS], preferred_element_type=f32)
            u += jnp.dot(rows, ubuf[slot, s * DS:(s + 1) * DS], preferred_element_type=f32)
        h = (g / (1.0 + jnp.exp(-g)) * u).astype(jnp.bfloat16)
        hid[:, pl.ds(pl.multiple_of(t * tf, tf), tf)] = h

        @pl.when(t + NG < NTF)
        def _():
            for cp in gcopy(t + NG):
                cp.start()

    loop(0, NTF, hidden_tile)

    def part(q):
        slot = lax.rem(q, ND)
        dcopy(q).wait()
        p = jnp.dot(hid[...], dbuf[slot], preferred_element_type=f32).astype(jnp.bfloat16)

        @pl.when(q + ND < nx * NT * CORES)
        def _():
            dcopy(q + ND).start()

        return p

    def c4(g):
        return rcopy(psend.at[g], prec.at[g], s4.at[g], r4.at[g], (mate, me))

    def c6(i, xi):
        dst = lax.rem(x + 1 + xi, nx) * CORES + c
        return rcopy(xsend.at[i], xrec.at[i], s6.at[i], r6.at[i], (dst, me))

    for xi in range(nx):
        base = xi * NT

        def pair(f, xi=xi, base=base):
            c4(base + f).wait_recv()
            total = pmine[base + f].astype(f32) + prec[base + f].astype(f32)
            if xi < nx - 1:
                xsend[base + f] = total.astype(jnp.bfloat16)
                c6(base + f, xi).start()
            else:
                own[f] = total

        def tile(f, base=base, pair=pair):
            g = base + f
            psend[g] = part(CORES * g)
            c4(g).start()
            pmine[g] = part(CORES * g + 1)

            @pl.when(f > 0)
            def _():
                pair(f - 1)

        loop(0, NT, tile)
        pair(NT - 1)

    def c5(f, k):
        dst = lax.rem(me + k, E)
        return rcopy(sumb.at[f, dst], ret.at[f, me], s5.at[f, k], r5.at[f, k], (sec, dst))

    def finish(f):
        total = own[f]
        for xi in range(nx - 1):
            c6(xi * NT + f, xi).wait_recv()
            total = total + xrec[xi * NT + f].astype(f32)
        sumb[f] = total.astype(jnp.bfloat16).reshape(E, C, ft)
        loop(1, E, lambda k: c5(f, k).start())
        ret[f, me] = sumb[f, me]

    loop(0, NT, finish)

    for f in range(NT):
        loop(1, E, lambda k: c5(f, k).wait())
        out[:, f * ft:(f + 1) * ft] = jnp.dot(
            weigh[...],
            ret[f].reshape(R, ft).astype(f32),
            precision=lax.Precision.HIGHEST,
            preferred_element_type=f32,
        ).astype(jnp.bfloat16)
    loop(0, nx * NT, lambda g: c4(g).wait_send())
    for xi in range(nx - 1):
        loop(0, NT, lambda f: c6(xi * NT + f, xi).wait_send())


def on_device(hidden_states, route_experts, route_weights, gate_weight, up_weight, down_weight):
    E = lax.axis_size("ep")
    S = lax.axis_size("section")
    tok_rows, D = hidden_states.shape
    FFS = gate_weight.shape[2]
    M = E // EXPERTS
    C = tok_rows // 2
    DS = D // S
    chosen = route_experts.reshape(-1)
    one_hot = (chosen[:, None] == jnp.arange(EXPERTS, dtype=jnp.int32)[None, :]).astype(jnp.int32)
    earlier = jnp.cumsum(one_hot, axis=0) - one_hot
    slot_index = jnp.sum(earlier * one_hot, axis=1)
    position = (chosen * C + slot_index).reshape(tok_rows, 2)
    columns = jnp.arange(EXPERTS * C, dtype=jnp.int32)
    matches = position[:, :, None] == columns[None, None, :]
    select = jnp.sum(matches.astype(jnp.int32), axis=1).astype(jnp.bfloat16)
    weighing = jnp.sum(matches.astype(jnp.float32) * route_weights[:, :, None], axis=1)
    mine = lax.dynamic_slice_in_dim(hidden_states, lax.axis_index("section") * DS, DS, 1)
    packed = jnp.einsum("tj,td->jd", select, mine, preferred_element_type=jnp.float32)
    packed = packed.astype(jnp.bfloat16).reshape(EXPERTS, C, DS)
    weigh = jnp.repeat(weighing.reshape(tok_rows, EXPERTS, C), M, axis=1).reshape(tok_rows, E * C)

    R = E * C
    nx = S // CORES
    ft = fit(DS, (512, 384, 256, 128))
    NT = DS // ft
    budget = 58_000_000 - (R * DS * 2 * (S + 3 * nx + 2 * nx + 4) + R * FFS * 2)
    tf = 256 if FFS % 256 == 0 and budget > 25_000_000 else 128
    NTF, NQ = FFS // tf, nx * NT * CORES
    gate_bytes, down_bytes = D * tf * 4, FFS * ft * 2
    ND = max(2, min(NQ, 6, budget // 4 // down_bytes))
    NG = max(2, min(NTF, (budget - ND * down_bytes) // gate_bytes))
    bf16, f32 = jnp.bfloat16, jnp.float32
    dma = pltpu.SemaphoreType.DMA
    nxs = max(1, nx - 1) * NT
    vmem = pl.BlockSpec(memory_space=pltpu.VMEM)
    hbm = pl.BlockSpec(memory_space=pl.ANY)
    return pl.pallas_call(
        functools.partial(kernel, E, S, C, D, FFS, tf, ft, NG, ND),
        out_shape=jax.ShapeDtypeStruct((tok_rows, DS), bf16),
        in_specs=[vmem, vmem, hbm, hbm, hbm],
        out_specs=vmem,
        scratch_shapes=[
            pltpu.VMEM((S, E, C, DS), bf16),
            pltpu.VMEM((NG, D, tf), bf16),
            pltpu.VMEM((NG, D, tf), bf16),
            pltpu.VMEM((ND, FFS, ft), bf16),
            pltpu.VMEM((R, FFS), bf16),
            pltpu.VMEM((nx * NT, R, ft), bf16),
            pltpu.VMEM((nx * NT, R, ft), bf16),
            pltpu.VMEM((nx * NT, R, ft), bf16),
            pltpu.VMEM((nxs, R, ft), bf16),
            pltpu.VMEM((nxs, R, ft), bf16),
            pltpu.VMEM((NT, R, ft), f32),
            pltpu.VMEM((NT, E, C, ft), bf16),
            pltpu.VMEM((NT, E, C, ft), bf16),
            dma((E,)), dma((E,)),
            dma((nx, E)), dma((nx, E)),
            dma((nx, E)), dma((nx, E)),
            dma((nx * NT,)), dma((nx * NT,)),
            dma((NT, E)), dma((NT, E)),
            dma((nxs,)), dma((nxs,)),
            dma((NG,)), dma((NG,)), dma((ND,)),
            dma(()),
        ],
        compiler_params=pltpu.CompilerParams(
            collective_id=0, has_side_effects=True, vmem_limit_bytes=67_043_328
        ),
    )(packed, weigh, gate_weight, up_weight, down_weight)


def solution(mesh):
    return jax.shard_map(
        on_device,
        mesh=mesh,
        in_specs=(
            P("ep", None),
            P("ep", None),
            P("ep", None),
            P("ep", None, "section"),
            P("ep", None, "section"),
            P("ep", "section", None),
        ),
        out_specs=P("ep", "section"),
        check_vma=False,
    )
```

time: 191 us -> 74.9 us (0.39)
  waiting for transfers between devices: 96.1 us -> 0 us
  Pallas kernels: 0 us -> 67.3 us
  matrix products: 35.2 us -> 2.06 us
  blocking collectives: 27.3 us -> 0 us
  between operations: 13.2 us -> 0.04 us
  local copies, waits for them, and re-layouts: 12.3 us -> 2.66 us
  starting transfers between devices: 5.6 us -> 0 us
    pallas_call x0 -> x1, Pallas kernels: none -> 67.3 us  [on_device(): pl.pallas_call(functools.partial(kernel, E, S, C, D, FFS, tf, ft, NG, ND)...]
    reduce_scatter x2 -> x0, waiting for transfers between devices: 53.1 us -> none  [the longest x1 33 us: on_device(): lax.psum_scatter(partials.astype(jnp.float32).astype(jnp.bfloat16), 'sect...]
    dot_general x4 -> x1, matrix products: 35.2 us -> 2.06 us  [on_device(): jnp.einsum('tj,td->jd', select, mine, preferred_element_type=jnp.float32)]
    all_to_all x1 -> x0, blocking collectives: 27.3 us -> none  [on_device(): lax.all_to_all(own_slots, 'ep', split_axis=0, concat_axis=0, tiled=True)]
    all_gather x1 -> x0, waiting for transfers between devices: 23.2 us -> none  [on_device(): lax.all_gather(arrived, 'section', axis=1, tiled=True)]
    all_to_all x1 -> x0, waiting for transfers between devices: 19.8 us -> none  [on_device(): lax.all_to_all(summed.astype(jnp.bfloat16), 'ep', split_axis=0, concat_ax...]
    all_to_all x1 -> x0, starting transfers between devices: 5.52 us -> none  [on_device(): lax.all_to_all(summed.astype(jnp.bfloat16), 'ep', split_axis=0, concat_ax...]
    reshape x1 -> x0, local copies, waits for them, and re-layouts: 4.35 us -> none  [expert_rows(): return result.reshape(sources, slot_count, features)]
  transfers between devices with their start and end apart: 4 -> 0, of which waited for: 4 -> 0; matrix products, arithmetic and copies ran while one was open for 0% -> 0% of each run, Pallas kernels for 0% -> 0%
where the time goes in v1:
time: 74.9 us; the launch traced here: 74.7 us
  Pallas kernels  67.3 us (90%)
  local copies, waits for them, and re-layouts  2.66 us (4%)
  other arithmetic  2.56 us (3%)
  matrix products  2.06 us (3%)
    pallas_call x1, Pallas kernels, on_device(): pl.pallas_call(functools.partial(kernel, E, S, C, D, FFS, tf, ft, NG, ND)...  67.3 us
    unnamed x2, local copies, waits for them, and re-layouts  2.34 us
    dot_general x1, matrix products, on_device(): jnp.einsum('tj,td->jd', select, mine, preferred_element_type=jnp.float32)  2.06 us

profile of v1, /device:TPU:0, one launch (start us, length us, event | category | flops | bytes accessed | tf_op | source)
XLA Modules:
  0.0 74.7 jit_solution(15439739722328391311)
XLA Ops:
  0.0 0.8 %copy.19 = s32[48,2]{1,0:T(8,128)S(1)} copy(s32[48,2]{0,1:T(2,128)} %param.7) | data formatting | bytes 768 | tf_op args[1]
  0.8 0.1 eq.28
  0.9 0.1 fusion.1
  1.0 0.1 reduce_window_sum.11
  1.1 0.2 select_reduce_fusion.1
  1.3 0.1 reduce_sum.30
  1.4 0.1 copy.20
  1.5 0.7 multiply_add_fusion
  2.2 1.4 %select_reduce_fusion.weigh = f32[48,192]{1,0:T(8,128)} fusion(f32[48,2]{0,1:T(2,128)} %param.8, s32[48,2]{0,1:T(2,128)S(1)} %multiply_add_fusion), kind=kLoop, calls=%fused_computation.2 | loop fusion | flops 46080 | bytes 37632 | tf_op jit(solution)/shard_map/reduce_sum | solution.py:243
  3.6 0.1 convert_reduce_fusion
  3.7 2.1 %convolution_convert_fusion = bf16[192,1536]{1,0:T(8,128)(2,1)} fusion(bf16[48,6144]{1,0:T(8,128)(2,1)} %param.6, s32[]{:T(128)S(6)} %select_n.3, s32[48,192]{1,0:T(8,128)S(1)} %convert_reduce_fusion), kind=kOutput, calls=%fused_computation | convolution fusion | flops 28615680 | bytes 774148 | tf_op jit(solution)/shard_map/tj,td->jd/dot_general | solution.py:245
  5.7 67.3 %shard_map.64 = bf16[48,1536]{1,0:T(8,128)(2,1)} custom-call(bf16[8,24,1536]{2,1,0:T(8,128)(2,1)} %bitcast.1, f32[48,192]{1,0:T(8,128)} %select_reduce_fusion.weigh, bf16[1,6144,2048]{2,1,0:T(8,128)(2,1)} %gate.1, bf16[1,6144,2048]{2,1,0:T(8,128)(2,1)} %up.1, bf16[1,2048,6144]{2,1,0:T(8,128)(2,1)} %down.1), custom_call_target="tpu_custom_call" | custom-call | tf_op jit(solution)/shard_map/pallas_call | solution.py:264
  73.1 1.6 %copy.22 = bf16[48,1536]{1,0:T(8,128)(2,1)} copy(bf16[48,1536]{1,0:T(8,128)(2,1)} %shard_map.64) | data formatting | bytes 294912
